TPU v7x, 32 devices: a whole 2x2x4 slice. The times are simulated.
32 devices in a mesh: batch: 8 (over y, x, core), head: 4 (over z).
Axes of the slice: x: 2, y: 2, z: 4, core: 2. Of those that a mesh axis runs over, the one named last changes fastest.
Arguments:
- inputs: bfloat16 [8, 128, 2048], P(None, 'batch', 'head'), parts along dimension 1, may hold values from -6 to 6
- in_weight: bfloat16 [2048, 4, 384], P(None, 'head'), may hold values from -0.125 to 0.125
- gate_weight: bfloat16 [2048, 4], P(None, 'head'), may hold values from -0.125 to 0.125
- gate_bias: float32 [4], P('head'), may hold values from -2 to 3
- norm_gain: float32 [512], P('head'), may hold values from 0.1 to 1.9
- out_weight: bfloat16 [512, 2048], P('head'), may hold values from -0.375 to 0.375
- inv_gram: float32 [128, 4, 128, 128], P('batch', 'head'), parts along dimension 0, may hold values from -17 to 17, as said below
- value_key: float32 [128, 4, 128, 128], P('batch', 'head'), parts along dimension 0, may hold values from -6 to 6
Outputs:
- layer_out: float32 [8, 128, 2048], P(None, 'batch', 'head'), parts along dimension 1
There are 8 independent parts, one for each index of `batch`. A program takes and returns all parts, laid end to end along the dimension named above; an argument that names none is the same for every part. Nothing has to cross between parts.
Inputs may be any that keep to these rules, and one draw needn't show every extreme that they name: `inv_gram`: each [128, 128] matrix is symmetric positive definite.
All inputs are finite; a program needn't handle non-finite values.
Results may differ from a plain program's by a relative error of at most 0.0029.
Values may be sent and summed in bfloat16 or wider, within the bound.
A program may use at most 64 MiB of HBM per device.

v0:
```python
import jax
import jax.numpy as jnp
from jax import lax
from jax.sharding import PartitionSpec as P


def advance(gram_inv, memory, projected, gate, gate_bias, head_size):
    batch_rows, local_heads = gate.shape
    pieces = projected.reshape(batch_rows, local_heads, 3 * head_size)
    queries = pieces[..., :head_size]
    keys_now = pieces[..., head_size : 2 * head_size]
    values_now = pieces[..., 2 * head_size :]
    forget = 0.8 + 0.2 * jax.nn.sigmoid(gate + gate_bias)
    keys_now = keys_now * lax.rsqrt(jnp.sum(keys_now * keys_now, axis=-1, keepdims=True) + 1e-06)
    queries = queries * lax.rsqrt(jnp.sum(queries * queries, axis=-1, keepdims=True) + 1e-06)
    gram_key = jnp.einsum("bhij,bhj->bhi", gram_inv, keys_now, precision=lax.Precision.HIGHEST)
    denominator = forget + jnp.sum(keys_now * gram_key, axis=-1)
    gram_inv = (
        gram_inv - gram_key[..., :, None] * gram_key[..., None, :] / denominator[..., None, None]
    ) / forget[..., None, None]
    memory = forget[..., None, None] * memory + values_now[..., :, None] * keys_now[..., None, :]
    gram_query = jnp.einsum("bhij,bhj->bhi", gram_inv, queries, precision=lax.Precision.HIGHEST)
    readout = jnp.einsum("bhij,bhj->bhi", memory, gram_query, precision=lax.Precision.HIGHEST)
    return (gram_inv, memory, readout.reshape(batch_rows, local_heads * head_size))


def local(inputs, in_weight, gate_weight, gate_bias, norm_gain, out_weight, inv_gram, value_key):
    step_count, batch_rows, _ = inputs.shape
    d_model = in_weight.shape[0]
    local_heads = in_weight.shape[1]
    head_size = in_weight.shape[2] // 3
    total_width = local_heads * head_size * lax.axis_size("head")
    weight_flat = in_weight.reshape(d_model, local_heads * 3 * head_size)
    gram_inv = inv_gram
    memory = value_key
    readouts = []
    for position in range(step_count):
        rows = lax.all_gather(inputs[position], "head", axis=1, tiled=True)
        projected = jnp.dot(rows, weight_flat, preferred_element_type=jnp.float32)
        gate = jnp.dot(rows, gate_weight, preferred_element_type=jnp.float32)
        gram_inv, memory, readout = advance(gram_inv, memory, projected, gate, gate_bias, head_size)
        readouts.append(readout)
    readout_all = jnp.stack(readouts, axis=0)
    squares = lax.psum(jnp.sum(readout_all * readout_all, axis=-1), "head")
    hidden = (
        norm_gain * readout_all * lax.rsqrt(squares / total_width + 1e-06)[:, :, None]
    ).astype(jnp.bfloat16)
    partial_out = jnp.dot(
        hidden.reshape(step_count * batch_rows, -1), out_weight, preferred_element_type=jnp.float32
    )
    partial_out = partial_out.reshape(step_count, batch_rows, d_model)
    return lax.psum_scatter(partial_out, "head", scatter_dimension=2, tiled=True)


def solution(mesh):
    in_specs = (
        P(None, "batch", "head"),
        P(None, "head", None),
        P(None, "head"),
        P("head"),
        P("head"),
        P("head", None),
        P("batch", "head", None, None),
        P("batch", "head", None, None),
    )
    out_specs = P(None, "batch", "head")
    return jax.shard_map(local, mesh=mesh, in_specs=in_specs, out_specs=out_specs, check_vma=False)
```

profile of v0, /device:TPU:0, one launch (start us, length us, event | category | flops | bytes accessed | tf_op | source)
XLA Modules:
  0.0 223.0 jit_solution(10314637504935739932)
XLA Ops:
  7.5 14.9 %all-gather = bf16[1,16,2048]{2,1,0:T(8,128)(2,1)S(1)} all-gather(bf16[1,16,512]{2,1,0:T(8,128)(2,1)S(1)} %get-tuple-element.27), channel_id=2, replica_groups=mesh['batch'=8,'head'=4] {'head'}, dimensions={2}, use_global_device_ids=true | all-gather | bytes 81920 | tf_op jit(solution)/shard_map/all_gather | solution.py:38
  23.0 1.7 fusion.132
  26.1 1.7 convolution_bitcast_fusion.7
  27.8 1.9 fusion.134
  29.7 13.3 %all-gather.1 = bf16[1,16,2048]{2,1,0:T(8,128)(2,1)S(1)} all-gather(bf16[1,16,512]{2,1,0:T(8,128)(2,1)S(1)} %get-tuple-element.26), channel_id=3, replica_groups=mesh['batch'=8,'head'=4] {'head'}, dimensions={2}, use_global_device_ids=true | all-gather | bytes 81920 | tf_op jit(solution)/shard_map/all_gather | solution.py:38
  43.4 13.2 %all-gather.3 = bf16[1,16,2048]{2,1,0:T(8,128)(2,1)S(1)} all-gather(bf16[1,16,512]{2,1,0:T(8,128)(2,1)S(1)} %get-tuple-element.24), channel_id=5, replica_groups=mesh['batch'=8,'head'=4] {'head'}, dimensions={2}, use_global_device_ids=true | all-gather | bytes 81920 | tf_op jit(solution)/shard_map/all_gather | solution.py:38
  57.2 13.4 %all-gather.2 = bf16[1,16,2048]{2,1,0:T(8,128)(2,1)S(1)} all-gather(bf16[1,16,512]{2,1,0:T(8,128)(2,1)S(1)} %get-tuple-element.25), channel_id=4, replica_groups=mesh['batch'=8,'head'=4] {'head'}, dimensions={2}, use_global_device_ids=true | all-gather | bytes 81920 | tf_op jit(solution)/shard_map/all_gather | solution.py:38
  71.2 1.7 fusion.129
  73.4 2.2 multiply_add_fusion.3
  75.6 1.7 convolution_bitcast_fusion.6
  77.4 2.1 fusion.127
  79.5 1.7 fusion.124
  83.5 2.6 %fusion.122 = f32[16,1,128]{2,1,0:T(1,128)S(1)} fusion(f32[16,128,1]{1,2,0:T(1,128)S(1)} %convolution_bitcast_fusion.5, f32[16,128]{1,0:T(8,128)S(1)} %bitcast.573, f32[16,128]{1,0:T(8,128)S(1)} %get-tuple-element.44, f32[16]{0:T(128)S(1)} %fusion.81, f32[16,1,128,128]{3,2,1,0:T(8,128)S(1)} %copy-done.2, f32[16,128]{1,0:T(8,128)S(1)} %bitcast.568, ...), kind=kOutput, calls=%fused_computation.122 | convolution fusion | flops 5505024 | bytes 1114304 | tf_op jit(solution)/shard_map/bhij,bhj->bhi/dot_general | solution.py:23
  86.1 1.7 fusion.119
  88.0 13.5 %all-gather.4 = bf16[1,16,2048]{2,1,0:T(8,128)(2,1)S(1)} all-gather(bf16[1,16,512]{2,1,0:T(8,128)(2,1)S(1)} %get-tuple-element.23), channel_id=6, replica_groups=mesh['batch'=8,'head'=4] {'head'}, dimensions={2}, use_global_device_ids=true | all-gather | bytes 81920 | tf_op jit(solution)/shard_map/all_gather | solution.py:38
  104.5 1.7 fusion.114
  106.4 13.1 %all-gather.5 = bf16[1,16,2048]{2,1,0:T(8,128)(2,1)S(1)} all-gather(bf16[1,16,512]{2,1,0:T(8,128)(2,1)S(1)} %get-tuple-element.22), channel_id=7, replica_groups=mesh['batch'=8,'head'=4] {'head'}, dimensions={2}, use_global_device_ids=true | all-gather | bytes 81920 | tf_op jit(solution)/shard_map/all_gather | solution.py:38
  121.3 1.7 convolution_bitcast_fusion.3
  123.2 1.7 fusion.109
  125.0 13.1 %all-gather.6 = bf16[1,16,2048]{2,1,0:T(8,128)(2,1)S(1)} all-gather(bf16[1,16,512]{2,1,0:T(8,128)(2,1)S(1)} %get-tuple-element.28), channel_id=8, replica_groups=mesh['batch'=8,'head'=4] {'head'}, dimensions={2}, use_global_device_ids=true | all-gather | bytes 81920 | tf_op jit(solution)/shard_map/all_gather | solution.py:38
  140.4 1.7 convolution_bitcast_fusion.2
  142.2 1.7 fusion.104
  144.1 13.5 %all-gather.7 = bf16[1,16,2048]{2,1,0:T(8,128)(2,1)S(1)} all-gather(bf16[1,16,512]{2,1,0:T(8,128)(2,1)S(1)} %get-tuple-element.21), channel_id=9, replica_groups=mesh['batch'=8,'head'=4] {'head'}, dimensions={2}, use_global_device_ids=true | all-gather | bytes 81920 | tf_op jit(solution)/shard_map/all_gather | solution.py:38
  158.1 2.0 subtract_divide_fusion
  161.9 1.7 fusion.99
  165.5 1.9 fusion.112
  167.4 2.1 fusion.107
  169.5 2.6 %fusion.102 = f32[16,1,128]{2,1,0:T(1,128)S(1)} fusion(f32[16,128,1]{1,2,0:T(1,128)S(1)} %convolution_bitcast_fusion.1, f32[16,128]{1,0:T(8,128)S(1)} %bitcast.579, f32[16,128]{1,0:T(8,128)S(1)} %get-tuple-element.32, f32[16]{0:T(128)S(1)} %get-tuple-element.64, f32[16,1,128,128]{3,2,1,0:T(8,128)S(1)} %get-tuple-element.53, f32[16,128]{1,0:T(8,128)S(1)} %bitcast.576, ...), kind=kOutput, calls=%fused_computation.102 | convolution fusion | flops 5505024 | bytes 1114304 | tf_op jit(solution)/shard_map/bhij,bhj->bhi/dot_general | solution.py:23
  172.3 1.9 convolution_bitcast_fusion
  174.2 3.3 %fusion.97 = f32[16,1,128]{2,1,0:T(1,128)S(1)} fusion(f32[16,128,1]{1,2,0:T(1,128)S(1)} %convolution_bitcast_fusion, f32[16,128]{1,0:T(8,128)S(1)} %bitcast.582, f32[16,128]{1,0:T(8,128)S(1)} %get-tuple-element.29, f32[16]{0:T(128)S(1)} %get-tuple-element.66, f32[16,128]{1,0:T(8,128)S(1)} %bitcast.580, f32[16,128]{1,0:T(8,128)S(1)} %get-tuple-element.32, ...), kind=kOutput, calls=%fused_computation.97 | convolution fusion | flops 6291456 | bytes 1130752 | tf_op jit(solution)/shard_map/bhij,bhj->bhi/dot_general | solution.py:23
  177.6 11.6 %psum.7 = f32[8,16]{1,0:T(8,128)S(1)} all-reduce(f32[8,16]{1,0:T(8,128)S(1)} %multiply_reduce_fusion), channel_id=1, replica_groups=mesh['batch'=8,'head'=4] {'head'}, use_global_device_ids=true, to_apply=%region_25.0 | all-reduce | flops 128 | bytes 1024 | tf_op jit(solution)/shard_map/psum | solution.py:44
  190.5 25.6 %reduce-scatter.2.cloned.1.call-done = f32[8,16,512]{2,1,0:T(8,128)} async-done(((f32[8,16,2048]{2,1,0:T(8,128)}), f32[8,16,512]{2,1,0:T(8,128)}) %reduce-scatter.2.cloned.1.call-update) | async-done | bytes 262160 | tf_op jit(solution)/shard_map/reduce_scatter | solution.py:52
  (85 shorter events, 20.1 us)
Async XLA Ops:
  6.5 15.9 %copy-start = (bf16[2048,1,384]{2,0,1:T(8,128)(2,1)S(1)}, bf16[2048,1,384]{2,0,1:T(8,128)(2,1)}, u32[]{:S(2)}) copy-start(bf16[2048,1,384]{2,0,1:T(8,128)(2,1)} %param.9) | copy-start | bytes 4718596
  6.5 16.4 %copy-start.1 = (f32[16,1,128,128]{3,2,1,0:T(8,128)S(1)}, f32[16,1,128,128]{3,2,1,0:T(8,128)}, u32[]{:S(2)}) copy-start(f32[16,1,128,128]{3,2,1,0:T(8,128)} %param.14) | copy-start | bytes 3145732
  6.5 19.0 %copy-start.5 = (bf16[2048,1]{0,1:T(2,128)(2,1)S(1)}, bf16[2048,1]{0,1:T(2,128)(2,1)}, u32[]{:S(2)}) copy-start(bf16[2048,1]{0,1:T(2,128)(2,1)} %param.10) | copy-start | bytes 12292
  6.5 209.6 %reduce-scatter.2.cloned.1.call-start = ((), (), s32[]{:S(2)}) async-start(), calls=%async_computation.1 | async-start | bytes 1310720 | tf_op jit(solution)/shard_map/reduce_scatter | solution.py:52
  25.7 2.1 copy-start.2
  174.2 15.0 %copy-start.3 = (bf16[128,2048]{1,0:T(8,128)(2,1)S(1)}, bf16[128,2048]{1,0:T(8,128)(2,1)}, u32[]{:S(2)}) copy-start(bf16[128,2048]{1,0:T(8,128)(2,1)} %param.13) | copy-start | bytes 1572868
  174.2 15.0 %copy-start.4 = (f32[128]{0:T(128)S(1)}, f32[128]{0:T(128)}, u32[]{:S(2)}) copy-start(f32[128]{0:T(128)} %param.12) | copy-start | bytes 1540
Sparse Core Ops, SparseCore 0:
  190.6 25.4 reduce-scatter.1
where the time goes:
time: 223 us
  blocking collectives  120 us (54%)
  matrix products  50.9 us (23%)
  waiting for transfers between devices  25.7 us (12%)
  between operations  14.4 us (6%)
  other arithmetic  11.4 us (5%)
    all_gather x8, blocking collectives, local(): rows = lax.all_gather(inputs[position], 'head', axis=1, tiled=True)  108 us
    reduce_scatter x1, waiting for transfers between devices, local(): lax.psum_scatter(partial_out, 'head', scatter_dimension=2, tiled=True)  25.6 us
    dot_general x8, matrix products, advance(): jnp.einsum('bhij,bhj->bhi', memory, gram_query, precision=lax.Precision.H...  18.2 us
    dot_general x8, matrix products, advance(): jnp.einsum('bhij,bhj->bhi', gram_inv, queries, precision=lax.Precision.HI...  13.9 us
    dot_general x8, matrix products, advance(): jnp.einsum('bhij,bhj->bhi', gram_inv, keys_now, precision=lax.Precision.H...  13.9 us
    psum x1, blocking collectives, local(): squares = lax.psum(jnp.sum(readout_all * readout_all, axis=-1), 'head')  11.6 us
    div x6, other arithmetic, advance(): (gram_inv - gram_key[..., :, None] * gram_key[..., None, :] / denominator...  6.41 us
  transfers between devices with their start and end apart: 1, of which 1 were waited for; matrix products, arithmetic and copies ran while one was open for 0% of the time, Pallas kernels for 0%

commit v1 on v0

v1 whole, which is shorter than its diff:
```python
import functools
import math

import jax
import jax.numpy as jnp
from jax import lax
from jax.experimental import pallas as pl
from jax.experimental.pallas import tpu as pltpu
from jax.sharding import PartitionSpec as P

MESH = pl.DeviceIdType.MESH
F32 = jnp.float32
BF16 = jnp.bfloat16
CHUNKS = 4
NT = (((1,), (1,)), ((), ()))


def split(x):
    hi = x.astype(BF16)
    lo = (x - hi.astype(F32)).astype(BF16)
    return hi, lo


def rowsum(x):
    return jnp.sum(x, axis=-1, keepdims=True)


def kernel(
    n,
    group,
    x_hbm,
    w_hbm,
    gate_hbm,
    bias_ref,
    gain_ref,
    ow_hbm,
    a_hbm,
    m_hbm,
    out_ref,
    xg,
    w,
    gate,
    a32,
    m32,
    a2,
    m2,
    wout,
    pacc,
    gacc,
    kbuf,
    qbuf,
    akbuf,
    aqbuf,
    wbuf,
    robuf,
    rbuf,
    sqbuf,
    lsem,
    xs,
    xr,
    w1s,
    w1r,
    w2s,
    w2r,
    rs,
    rr,
    qs,
    qr,
):
    steps, seqs, feats = x_hbm.shape
    rows = steps * seqs
    heads_rows = ow_hbm.shape[0]
    cols = ow_hbm.shape[1] // n
    size = a_hbm.shape[1]
    me = lax.axis_index("head")
    b = lax.axis_index("batch")
    mine = lax.rem(b, group)
    base = b - mine
    slab = heads_rows // group
    span = steps // CHUNKS

    loads = [
        pltpu.make_async_copy(x_hbm, xg.at[me], lsem.at[0]),
        pltpu.make_async_copy(w_hbm, w, lsem.at[1]),
        pltpu.make_async_copy(gate_hbm, gate, lsem.at[2]),
        pltpu.make_async_copy(a_hbm, a32, lsem.at[3]),
        pltpu.make_async_copy(m_hbm, m32, lsem.at[4]),
        pltpu.make_async_copy(
            ow_hbm.at[:, pl.ds(pl.multiple_of(me * cols, cols), cols)], wout.at[me], lsem.at[5]
        ),
    ]
    for load in loads:
        load.start()

    barrier = pltpu.get_barrier_semaphore()

    @pl.when(me > 0)
    def _():
        pl.semaphore_signal(barrier, inc=1, device_id={"head": me - 1}, device_id_type=MESH)

    @pl.when(me < n - 1)
    def _():
        pl.semaphore_signal(barrier, inc=1, device_id={"head": me + 1}, device_id_type=MESH)

    for o in range(1, group):
        peer = base + lax.rem(mine + o, group)
        pl.semaphore_signal(barrier, inc=1, device_id={"batch": peer}, device_id_type=MESH)
    inner = jnp.logical_and(me > 0, me < n - 1)

    @pl.when(inner)
    def _():
        pl.semaphore_wait(barrier, group + 1)

    @pl.when(jnp.logical_not(inner))
    def _():
        pl.semaphore_wait(barrier, group)

    def xcopy(j, c, way):
        part = xg.at[j, pl.ds(c * span, span)]
        return pltpu.make_async_remote_copy(
            src_ref=part,
            dst_ref=part,
            send_sem=xs.at[way, j, c],
            recv_sem=xr.at[j, c],
            device_id={"head": me + 1 if way == 0 else me - 1},
            device_id_type=MESH,
        )

    def forward(j, c):
        @pl.when(me < n - 1)
        def _():
            xcopy(j, c, 0).start()

    def backward(j, c):
        @pl.when(me > 0)
        def _():
            xcopy(j, c, 1).start()

    loads[0].wait()
    for c in range(CHUNKS):
        forward(me, c)
        backward(me, c)

    def project(j, first):
        x = xg[j].reshape(rows, feats)
        at = pl.ds(pl.multiple_of(j * feats, feats), feats)
        part = jnp.dot(x, w[at, :], preferred_element_type=F32)
        g = jnp.broadcast_to(gate[:, at].astype(F32), (size, feats)).astype(BF16)
        gpart = lax.dot_general(x, g, NT, preferred_element_type=F32)
        if first:
            pacc[...] = part
            gacc[...] = gpart
        else:
            pacc[...] += part
            gacc[...] += gpart

    loads[1].wait()
    loads[2].wait()
    project(me, True)
    loads[3].wait()
    for s in range(seqs):
        hi, lo = split(a32[s])
        a2[s, :size, :] = hi
        a2[s, size:, :] = lo
    loads[4].wait()

    def prepare(start, stop):
        for s in range(start, stop):
            hi, lo = split(m32[s].T)
            m2[s, :size, :] = hi
            m2[s, size:, :] = lo

    per = -(-seqs // max(n - 1, 1))
    for d in range(1, n):
        for c in range(CHUNKS):

            @pl.when(me >= d)
            def _():
                xcopy(me - d, c, 0).wait_recv()
                forward(me - d, c)

            @pl.when(me + d < n)
            def _():
                xcopy(me + d, c, 0).wait_recv()
                backward(me + d, c)

        @pl.when(me >= d)
        def _():
            project(me - d, False)

        @pl.when(me + d < n)
        def _():
            project(me + d, False)

        if d < n - 1 or n == 2:
            prepare(seqs * (d - 1) // max(n - 2, 1), seqs * d // max(n - 2, 1))

    def w1copy(o):
        other = lax.rem(me + o, n)
        return pltpu.make_async_remote_copy(
            src_ref=ow_hbm.at[
                pl.ds(pl.multiple_of(mine * slab, slab), slab),
                pl.ds(pl.multiple_of(other * cols, cols), cols),
            ],
            dst_ref=wout.at[me, pl.ds(pl.multiple_of(mine * slab, slab), slab)],
            send_sem=w1s.at[o],
            recv_sem=w1r.at[o],
            device_id={"head": other},
            device_id_type=MESH,
        )

    for o in range(1, n):
        w1copy(o).start()

    p = pacc[...]
    f = 0.8 + 0.2 * jax.nn.sigmoid(gacc[...] + bias_ref[...])
    q = p[:, :size]
    k = p[:, size : 2 * size]
    v = p[:, 2 * size :]
    k = k * lax.rsqrt(rowsum(k * k) + 1e-06)
    q = q * lax.rsqrt(rowsum(q * q) + 1e-06)
    kbuf[...] = k
    qbuf[...] = q
    for s in range(seqs):
        at = pl.ds(s, steps, stride=seqs)
        hi, lo = split(jnp.concatenate([kbuf[at, :], qbuf[at, :]], axis=0))
        left = jnp.concatenate(
            [jnp.concatenate([hi, hi], axis=1), jnp.concatenate([lo, lo], axis=1)], axis=0
        )
        r = jnp.dot(left, a2[s], preferred_element_type=F32)
        r = r[: 2 * steps] + r[2 * steps :]
        akbuf[at, :] = r[:steps]
        aqbuf[at, :] = r[steps:]

    def piece(x, t):
        return x[t * seqs : (t + 1) * seqs]

    ks = [piece(k, t) for t in range(steps)]
    qs_ = [piece(q, t) for t in range(steps)]
    vs = [piece(v, t) for t in range(steps)]
    fs = [piece(f, t) for t in range(steps)]
    ak = [akbuf[t * seqs : (t + 1) * seqs, :] for t in range(steps)]
    aq = [aqbuf[t * seqs : (t + 1) * seqs, :] for t in range(steps)]
    ws = []
    for t in range(steps):
        u = ak[t]
        rd = 1.0 / (fs[t] + rowsum(ks[t] * u))
        rf = 1.0 / fs[t]
        for i in range(t + 1, steps):
            ak[i] = (ak[i] - u * (rowsum(u * ks[i]) * rd)) * rf
        for i in range(t, steps):
            aq[i] = (aq[i] - u * (rowsum(u * qs_[i]) * rd)) * rf
        ws.append(aq[t])
        wbuf[t * seqs : (t + 1) * seqs, :] = aq[t]

    for s in range(seqs):
        at = pl.ds(s, steps, stride=seqs)
        hi, lo = split(wbuf[at, :])
        hi, lo = hi.astype(F32), lo.astype(F32)
        left = jnp.concatenate(
            [jnp.concatenate([hi, hi], axis=1), jnp.concatenate([lo, lo], axis=1)], axis=0
        ).astype(BF16)
        r = jnp.dot(left, m2[s], preferred_element_type=F32)
        robuf[at, :] = r[:steps] + r[steps:]

    decay = []
    whole = None
    pieces = []
    for t in range(steps):
        decay = [x * fs[t] for x in decay] + [None]
        whole = fs[t] if whole is None else whole * fs[t]
        total = whole * robuf[t * seqs : (t + 1) * seqs, :]
        for i in range(t + 1):
            e = rowsum(ks[i] * ws[t])
            total = total + (e * vs[i] if decay[i] is None else (e * decay[i]) * vs[i])
        decay[t] = jnp.ones_like(fs[t])
        pieces.append(total)
    ro = jnp.concatenate(pieces, axis=0)
    hi, lo = split(ro * ro)
    sqbuf[me] = lax.dot_general(
        jnp.ones((8, 2 * size), BF16),
        jnp.concatenate([hi, lo], axis=1),
        NT,
        preferred_element_type=F32,
    )
    rbuf[me] = (gain_ref[...] * ro).astype(BF16)

    def share(buf, send, recv, o):
        return pltpu.make_async_remote_copy(
            src_ref=buf.at[me],
            dst_ref=buf.at[me],
            send_sem=send.at[o],
            recv_sem=recv.at[o],
            device_id={"head": lax.rem(me + o, n)},
            device_id_type=MESH,
        )

    rcopy = functools.partial(share, rbuf, rs, rr)
    qcopy = functools.partial(share, sqbuf, qs, qr)
    for o in range(1, n):
        rcopy(o).start()
        qcopy(o).start()

    def w2copy(o, i):
        source = lax.rem(me + n - o, n)
        part = wout.at[source, pl.ds(pl.multiple_of(mine * slab, slab), slab)]
        return pltpu.make_async_remote_copy(
            src_ref=part,
            dst_ref=part,
            send_sem=w2s.at[o, i],
            recv_sem=w2r.at[o, i],
            device_id={"batch": base + lax.rem(mine + i, group)},
            device_id_type=MESH,
        )

    for o in range(1, n):
        w1copy(o).wait_recv()
        for i in range(1, group):
            w2copy(o, i).start()

    loads[5].wait()
    acc = jnp.dot(rbuf[me], wout[me], preferred_element_type=F32)
    squares = sqbuf[me]
    for o in range(1, n):
        source = lax.rem(me + n - o, n)
        rcopy(o).wait_recv()
        qcopy(o).wait_recv()
        for i in range(1, group):
            w2copy(o, i).wait_recv()
        acc = acc + jnp.dot(rbuf[source], wout[source], preferred_element_type=F32)
        squares = squares + sqbuf[source]
    scale = lax.rsqrt(squares[:1] / (n * size) + 1e-06)
    scale = jnp.broadcast_to(scale, (size, rows)).T
    for at in range(0, cols, size):
        out_ref[:, at : at + size] = acc[:, at : at + size] * scale

    for d in range(n):
        for c in range(CHUNKS):

            @pl.when(jnp.logical_and(me >= d, me < n - 1))
            def _():
                xcopy(me - d, c, 0).wait_send()

            @pl.when(jnp.logical_and(me + d < n, me > 0))
            def _():
                xcopy(me + d, c, 1).wait_send()

    for o in range(1, n):
        w1copy(o).wait_send()
        rcopy(o).wait_send()
        qcopy(o).wait_send()
        for i in range(1, group):
            w2copy(o, i).wait_send()


def local(n, batch, inputs, in_weight, gate_weight, gate_bias, norm_gain, out_weight, inv_gram, value_key):
    steps, seqs, feats = inputs.shape
    d_model, heads, width = in_weight.shape
    size = width // 3
    rows = steps * seqs
    cols = out_weight.shape[1] // n
    assert heads == 1
    group = math.gcd(math.gcd(batch, 8), out_weight.shape[0] // 16)
    anywhere = pl.BlockSpec(memory_space=pl.ANY)
    vmem = pl.BlockSpec(memory_space=pltpu.VMEM)
    dma = pltpu.SemaphoreType.DMA
    out = pl.pallas_call(
        functools.partial(kernel, n, group),
        out_shape=jax.ShapeDtypeStruct((rows, cols), F32),
        in_specs=[
            anywhere,
            anywhere,
            anywhere,
            vmem,
            vmem,
            anywhere,
            anywhere,
            anywhere,
        ],
        out_specs=vmem,
        scratch_shapes=[
            pltpu.VMEM((n, steps, seqs, feats), BF16),
            pltpu.VMEM((d_model, width), BF16),
            pltpu.VMEM((1, d_model), BF16),
            pltpu.VMEM((seqs, size, size), F32),
            pltpu.VMEM((seqs, size, size), F32),
            pltpu.VMEM((seqs, 2 * size, size), BF16),
            pltpu.VMEM((seqs, 2 * size, size), BF16),
            pltpu.VMEM((n, out_weight.shape[0], cols), BF16),
            pltpu.VMEM((rows, width), F32),
            pltpu.VMEM((rows, size), F32),
            pltpu.VMEM((rows, size), F32),
            pltpu.VMEM((rows, size), F32),
            pltpu.VMEM((rows, size), F32),
            pltpu.VMEM((rows, size), F32),
            pltpu.VMEM((rows, size), F32),
            pltpu.VMEM((rows, size), F32),
            pltpu.VMEM((n, rows, size), BF16),
            pltpu.VMEM((n, 8, rows), F32),
            dma((6,)),
            dma((2, n, CHUNKS)),
            dma((n, CHUNKS)),
            dma((n,)),
            dma((n,)),
            dma((n, group)),
            dma((n, group)),
            dma((n,)),
            dma((n,)),
            dma((n,)),
            dma((n,)),
        ],
        compiler_params=pltpu.CompilerParams(collective_id=0, has_side_effects=True),
    )(
        inputs,
        in_weight.reshape(d_model, width),
        gate_weight.reshape(1, d_model),
        gate_bias.reshape(1, 1),
        norm_gain.reshape(1, size),
        out_weight,
        inv_gram.reshape(seqs, size, size),
        value_key.reshape(seqs, size, size),
    )
    return out.reshape(steps, seqs, cols)


def solution(mesh):
    in_specs = (
        P(None, "batch", "head"),
        P(None, "head", None),
        P(None, "head"),
        P("head"),
        P("head"),
        P("head", None),
        P("batch", "head", None, None),
        P("batch", "head", None, None),
    )
    out_specs = P(None, "batch", "head")
    return jax.shard_map(
        functools.partial(local, mesh.shape["head"], mesh.shape["batch"]),
        mesh=mesh,
        in_specs=in_specs,
        out_specs=out_specs,
        check_vma=False,
    )
```

time: 223 us -> 30.1 us (0.13)
  blocking collectives: 120 us -> 0 us
  matrix products: 50.9 us -> 0 us
  Pallas kernels: 0 us -> 27.6 us
  waiting for transfers between devices: 25.7 us -> 0 us
  between operations: 14.4 us -> 0.66 us
  other arithmetic: 11.4 us -> 0 us
    all_gather x8 -> x0, blocking collectives: 108 us -> none  [local(): rows = lax.all_gather(inputs[position], 'head', axis=1, tiled=True)]
    dot_general x41 -> x0, matrix products: 50.9 us -> none  [the longest x8 18.2 us: advance(): jnp.einsum('bhij,bhj->bhi', memory, gram_query, precision=lax.Precision.H...]
    pallas_call x0 -> x1, Pallas kernels: none -> 27.6 us  [local(): pl.pallas_call(functools.partial(kernel, n, group), out_shape=jax.ShapeDt...]
    reduce_scatter x1 -> x0, waiting for transfers between devices: 25.6 us -> none  [local(): lax.psum_scatter(partial_out, 'head', scatter_dimension=2, tiled=True)]
    psum x1 -> x0, blocking collectives: 11.6 us -> none  [local(): squares = lax.psum(jnp.sum(readout_all * readout_all, axis=-1), 'head')]
    div x6 -> x0, other arithmetic: 6.41 us -> none  [advance(): (gram_inv - gram_key[..., :, None] * gram_key[..., None, :] / denominator...]
    add x3 -> x0, other arithmetic: 2.23 us -> none  [the longest x1 2.22 us: advance(): forget[..., None, None] * memory]
  transfers between devices with their start and end apart: 1 -> 0, of which waited for: 1 -> 0; matrix products, arithmetic and copies ran while one was open for 0% -> 0% of each run, Pallas kernels for 0% -> 0%
where the time goes in v1:
time: 30.1 us; the launch traced here: 30 us
  Pallas kernels  27.6 us (92%)
  local copies, waits for them, and re-layouts  1.67 us (6%)
  between operations  0.66 us (2%)
    pallas_call x1, Pallas kernels, local(): pl.pallas_call(functools.partial(kernel, n, group), out_shape=jax.ShapeDt...  27.6 us
    unnamed x1, local copies, waits for them, and re-layouts  1.67 us

profile of v1, /device:TPU:0, one launch (start us, length us, event | category | flops | bytes accessed | tf_op | source)
XLA Modules:
  0.0 30.0 jit_solution(4283457570276275907)
XLA Ops:
  0.7 27.6 %shard_map.82 = f32[128,512]{1,0:T(8,128)} custom-call(bf16[8,16,512]{2,1,0:T(8,128)(2,1)} %x_hbm.1, bf16[2048,384]{1,0:T(8,128)(2,1)} %bitcast.8, bf16[1,2048]{1,0:T(2,128)(2,1)} %bitcast.12, f32[1,1]{1,0:T(1,128)} %bitcast.7.bias_ref, f32[1,128]{1,0:T(1,128)} %bitcast.13, bf16[128,2048]{1,0:T(8,128)(2,1)} %ow_hbm.1, f32[16,128,128]{2,1,0:T(8,128)} %bitcast.9, ...), custom_call_target="tpu_custom_call" | custom-call | tf_op jit(solution)/shard_map/pallas_call | solution.py:367
  28.3 1.7 %copy.11 = f32[8,16,512]{2,1,0:T(8,128)} copy(f32[8,16,512]{2,1,0:T(8,128)} %bitcast.11) | data formatting | bytes 524288

commit v2 on v1

--- a/solution.py
+++ b/solution.py
@@ -11,7 +11,6 @@
 MESH = pl.DeviceIdType.MESH
 F32 = jnp.float32
 BF16 = jnp.bfloat16
-CHUNKS = 4
 NT = (((1,), (1,)), ((), ()))
 
 
@@ -77,7 +76,6 @@
     mine = lax.rem(b, group)
     base = b - mine
     slab = heads_rows // group
-    span = steps // CHUNKS
 
     loads = [
         pltpu.make_async_copy(x_hbm, xg.at[me], lsem.at[0]),
@@ -94,52 +92,47 @@
 
     barrier = pltpu.get_barrier_semaphore()
 
-    @pl.when(me > 0)
-    def _():
-        pl.semaphore_signal(barrier, inc=1, device_id={"head": me - 1}, device_id_type=MESH)
-
-    @pl.when(me < n - 1)
-    def _():
-        pl.semaphore_signal(barrier, inc=1, device_id={"head": me + 1}, device_id_type=MESH)
-
+    for o in range(1, n):
+        pl.semaphore_signal(
+            barrier, inc=1, device_id={"head": lax.rem(me + o, n)}, device_id_type=MESH
+        )
     for o in range(1, group):
         peer = base + lax.rem(mine + o, group)
         pl.semaphore_signal(barrier, inc=1, device_id={"batch": peer}, device_id_type=MESH)
-    inner = jnp.logical_and(me > 0, me < n - 1)
-
-    @pl.when(inner)
-    def _():
-        pl.semaphore_wait(barrier, group + 1)
-
-    @pl.when(jnp.logical_not(inner))
-    def _():
-        pl.semaphore_wait(barrier, group)
-
-    def xcopy(j, c, way):
-        part = xg.at[j, pl.ds(c * span, span)]
+    pl.semaphore_wait(barrier, n + group - 2)
+
+    order = sorted(range(1, n), key=lambda o: -min(o, n - o))
+
+    def xcopy(o):
         return pltpu.make_async_remote_copy(
-            src_ref=part,
-            dst_ref=part,
-            send_sem=xs.at[way, j, c],
-            recv_sem=xr.at[j, c],
-            device_id={"head": me + 1 if way == 0 else me - 1},
+            src_ref=xg.at[me],
+            dst_ref=xg.at[me],
+            send_sem=xs.at[o],
+            recv_sem=xr.at[o],
+            device_id={"head": lax.rem(me + o, n)},
             device_id_type=MESH,
         )
 
-    def forward(j, c):
-        @pl.when(me < n - 1)
-        def _():
-            xcopy(j, c, 0).start()
-
-    def backward(j, c):
-        @pl.when(me > 0)
-        def _():
-            xcopy(j, c, 1).start()
-
     loads[0].wait()
-    for c in range(CHUNKS):
-        forward(me, c)
-        backward(me, c)
+    for o in order:
+        xcopy(o).start()
+
+    def w1copy(o):
+        other = lax.rem(me + o, n)
+        return pltpu.make_async_remote_copy(
+            src_ref=ow_hbm.at[
+                pl.ds(pl.multiple_of(mine * slab, slab), slab),
+                pl.ds(pl.multiple_of(other * cols, cols), cols),
+            ],
+            dst_ref=wout.at[me, pl.ds(pl.multiple_of(mine * slab, slab), slab)],
+            send_sem=w1s.at[o],
+            recv_sem=w1r.at[o],
+            device_id={"head": other},
+            device_id_type=MESH,
+        )
+
+    for o in range(1, n):
+        w1copy(o).start()
 
     def project(j, first):
         x = xg[j].reshape(rows, feats)
@@ -170,47 +163,10 @@
             m2[s, :size, :] = hi
             m2[s, size:, :] = lo
 
-    per = -(-seqs // max(n - 1, 1))
-    for d in range(1, n):
-        for c in range(CHUNKS):
-
-            @pl.when(me >= d)
-            def _():
-                xcopy(me - d, c, 0).wait_recv()
-                forward(me - d, c)
-
-            @pl.when(me + d < n)
-            def _():
-                xcopy(me + d, c, 0).wait_recv()
-                backward(me + d, c)
-
-        @pl.when(me >= d)
-        def _():
-            project(me - d, False)
-
-        @pl.when(me + d < n)
-        def _():
-            project(me + d, False)
-
-        if d < n - 1 or n == 2:
-            prepare(seqs * (d - 1) // max(n - 2, 1), seqs * d // max(n - 2, 1))
-
-    def w1copy(o):
-        other = lax.rem(me + o, n)
-        return pltpu.make_async_remote_copy(
-            src_ref=ow_hbm.at[
-                pl.ds(pl.multiple_of(mine * slab, slab), slab),
-                pl.ds(pl.multiple_of(other * cols, cols), cols),
-            ],
-            dst_ref=wout.at[me, pl.ds(pl.multiple_of(mine * slab, slab), slab)],
-            send_sem=w1s.at[o],
-            recv_sem=w1r.at[o],
-            device_id={"head": other},
-            device_id_type=MESH,
-        )
-
-    for o in range(1, n):
-        w1copy(o).start()
+    for at, o in enumerate(order):
+        xcopy(o).wait_recv()
+        project(lax.rem(me + n - o, n), False)
+        prepare(seqs * at // (n - 1), seqs * (at + 1) // (n - 1))
 
     p = pacc[...]
     f = 0.8 + 0.2 * jax.nn.sigmoid(gacc[...] + bias_ref[...])
@@ -252,6 +208,23 @@
             aq[i] = (aq[i] - u * (rowsum(u * qs_[i]) * rd)) * rf
         ws.append(aq[t])
         wbuf[t * seqs : (t + 1) * seqs, :] = aq[t]
+
+    def w2copy(o, i):
+        source = lax.rem(me + n - o, n)
+        part = wout.at[source, pl.ds(pl.multiple_of(mine * slab, slab), slab)]
+        return pltpu.make_async_remote_copy(
+            src_ref=part,
+            dst_ref=part,
+            send_sem=w2s.at[o, i],
+            recv_sem=w2r.at[o, i],
+            device_id={"batch": base + lax.rem(mine + i, group)},
+            device_id_type=MESH,
+        )
+
+    for o in range(1, n):
+        w1copy(o).wait_recv()
+        for i in range(1, group):
+            w2copy(o, i).start()
 
     for s in range(seqs):
         at = pl.ds(s, steps, stride=seqs)
@@ -301,23 +274,6 @@
         rcopy(o).start()
         qcopy(o).start()
 
-    def w2copy(o, i):
-        source = lax.rem(me + n - o, n)
-        part = wout.at[source, pl.ds(pl.multiple_of(mine * slab, slab), slab)]
-        return pltpu.make_async_remote_copy(
-            src_ref=part,
-            dst_ref=part,
-            send_sem=w2s.at[o, i],
-            recv_sem=w2r.at[o, i],
-            device_id={"batch": base + lax.rem(mine + i, group)},
-            device_id_type=MESH,
-        )
-
-    for o in range(1, n):
-        w1copy(o).wait_recv()
-        for i in range(1, group):
-            w2copy(o, i).start()
-
     loads[5].wait()
     acc = jnp.dot(rbuf[me], wout[me], preferred_element_type=F32)
     squares = sqbuf[me]
@@ -334,18 +290,8 @@
     for at in range(0, cols, size):
         out_ref[:, at : at + size] = acc[:, at : at + size] * scale
 
-    for d in range(n):
-        for c in range(CHUNKS):
-
-            @pl.when(jnp.logical_and(me >= d, me < n - 1))
-            def _():
-                xcopy(me - d, c, 0).wait_send()
-
-            @pl.when(jnp.logical_and(me + d < n, me > 0))
-            def _():
-                xcopy(me + d, c, 1).wait_send()
-
-    for o in range(1, n):
+    for o in range(1, n):
+        xcopy(o).wait_send()
         w1copy(o).wait_send()
         rcopy(o).wait_send()
         qcopy(o).wait_send()
@@ -398,8 +344,8 @@
             pltpu.VMEM((n, rows, size), BF16),
             pltpu.VMEM((n, 8, rows), F32),
             dma((6,)),
-            dma((2, n, CHUNKS)),
-            dma((n, CHUNKS)),
+            dma((n,)),
+            dma((n,)),
             dma((n,)),
             dma((n,)),
             dma((n, group)),

time: 30.1 us -> 29.9 us (level)
  no operation moved by 1% of the time
where the time goes in v2:
time: 29.9 us; the launch traced here: 29.8 us
  Pallas kernels  27.4 us (92%)
  local copies, waits for them, and re-layouts  1.67 us (6%)
  between operations  0.66 us (2%)
    pallas_call x1, Pallas kernels, local(): pl.pallas_call(functools.partial(kernel, n, group), out_shape=jax.ShapeDt...  27.4 us
    unnamed x1, local copies, waits for them, and re-layouts  1.67 us

profile of v2, /device:TPU:0, one launch (start us, length us, event | category | flops | bytes accessed | tf_op | source)
XLA Modules:
  0.0 29.8 jit_solution(4868939200107946970)
XLA Ops:
  0.7 27.4 %shard_map.82 = f32[128,512]{1,0:T(8,128)} custom-call(bf16[8,16,512]{2,1,0:T(8,128)(2,1)} %x_hbm.1, bf16[2048,384]{1,0:T(8,128)(2,1)} %bitcast.8, bf16[1,2048]{1,0:T(2,128)(2,1)} %bitcast.12, f32[1,1]{1,0:T(1,128)} %bitcast.7.bias_ref, f32[1,128]{1,0:T(1,128)} %bitcast.13, bf16[128,2048]{1,0:T(8,128)(2,1)} %ow_hbm.1, f32[16,128,128]{2,1,0:T(8,128)} %bitcast.9, ...), custom_call_target="tpu_custom_call" | custom-call | tf_op jit(solution)/shard_map/pallas_call | solution.py:313
  28.1 1.7 %copy.11 = f32[8,16,512]{2,1,0:T(8,128)} copy(f32[8,16,512]{2,1,0:T(8,128)} %bitcast.11) | data formatting | bytes 524288

commit v3 on v2

v3 whole, which is shorter than its diff:
```python
import functools
import math

import jax
import jax.numpy as jnp
from jax import lax
from jax.experimental import pallas as pl
from jax.experimental.pallas import tpu as pltpu
from jax.sharding import PartitionSpec as P

MESH = pl.DeviceIdType.MESH
F32 = jnp.float32
BF16 = jnp.bfloat16
HALVES = 2
NT = (((1,), (1,)), ((), ()))


def split(x):
    hi = x.astype(BF16)
    lo = (x - hi.astype(F32)).astype(BF16)
    return hi, lo


def rowsum(x):
    return jnp.sum(x, axis=-1, keepdims=True)


def kernel(
    n,
    group,
    x_hbm,
    w_hbm,
    gate_hbm,
    bias_ref,
    gain_ref,
    ow_hbm,
    a_hbm,
    m_hbm,
    out_ref,
    xg,
    w,
    gate,
    a32,
    m32,
    a2,
    m2,
    wout,
    pacc,
    gacc,
    kbuf,
    qbuf,
    akbuf,
    aqbuf,
    wbuf,
    robuf,
    rbuf,
    sqbuf,
    lsem,
    xs,
    xr,
    w1s,
    w1r,
    w2s,
    w2r,
    rs,
    rr,
    qs,
    qr,
):
    steps, seqs, feats = x_hbm.shape
    rows = steps * seqs
    heads_rows = ow_hbm.shape[0]
    cols = ow_hbm.shape[1] // n
    size = a_hbm.shape[1]
    me = lax.axis_index("head")
    b = lax.axis_index("batch")
    mine = lax.rem(b, group)
    base = b - mine
    slab = heads_rows // group

    loads = [
        pltpu.make_async_copy(x_hbm, xg.at[me], lsem.at[0]),
        pltpu.make_async_copy(w_hbm, w, lsem.at[1]),
        pltpu.make_async_copy(gate_hbm, gate, lsem.at[2]),
        pltpu.make_async_copy(a_hbm, a32, lsem.at[3]),
        pltpu.make_async_copy(m_hbm, m32, lsem.at[4]),
        pltpu.make_async_copy(
            ow_hbm.at[:, pl.ds(pl.multiple_of(me * cols, cols), cols)], wout.at[me], lsem.at[5]
        ),
    ]
    for load in loads:
        load.start()

    barrier = pltpu.get_barrier_semaphore()

    for o in range(1, n):
        pl.semaphore_signal(
            barrier, inc=1, device_id={"head": lax.rem(me + o, n)}, device_id_type=MESH
        )
    for o in range(1, group):
        peer = base + lax.rem(mine + o, group)
        pl.semaphore_signal(barrier, inc=1, device_id={"batch": peer}, device_id_type=MESH)
    pl.semaphore_wait(barrier, n + group - 2)

    order = sorted(range(1, n), key=lambda o: -min(o, n - o))

    part = steps // HALVES
    band = part * seqs

    def xcopy(o, h):
        block = xg.at[me, pl.ds(h * part, part)]
        return pltpu.make_async_remote_copy(
            src_ref=block,
            dst_ref=block,
            send_sem=xs.at[o, h],
            recv_sem=xr.at[o, h],
            device_id={"head": lax.rem(me + o, n)},
            device_id_type=MESH,
        )

    loads[0].wait()
    for h in range(HALVES):
        for o in order:
            xcopy(o, h).start()

    def w1copy(o):
        other = lax.rem(me + o, n)
        return pltpu.make_async_remote_copy(
            src_ref=ow_hbm.at[
                pl.ds(pl.multiple_of(mine * slab, slab), slab),
                pl.ds(pl.multiple_of(other * cols, cols), cols),
            ],
            dst_ref=wout.at[me, pl.ds(pl.multiple_of(mine * slab, slab), slab)],
            send_sem=w1s.at[o],
            recv_sem=w1r.at[o],
            device_id={"head": other},
            device_id_type=MESH,
        )

    for o in range(1, n):
        w1copy(o).start()

    def project(j, h, first):
        x = xg[j, h * part : (h + 1) * part].reshape(band, feats)
        own = slice(h * band, (h + 1) * band)
        at = pl.ds(pl.multiple_of(j * feats, feats), feats)
        partial = jnp.dot(x, w[at, :], preferred_element_type=F32)
        g = jnp.broadcast_to(gate[:, at].astype(F32), (size, feats)).astype(BF16)
        gpart = lax.dot_general(x, g, NT, preferred_element_type=F32)
        if first:
            pacc[own, :] = partial
            gacc[own, :] = gpart
        else:
            pacc[own, :] += partial
            gacc[own, :] += gpart

    loads[1].wait()
    loads[2].wait()
    for h in range(HALVES):
        project(me, h, True)
    loads[3].wait()
    for s in range(seqs):
        hi, lo = split(a32[s])
        a2[s, :size, :] = hi
        a2[s, size:, :] = lo
    loads[4].wait()

    def prepare(start, stop):
        for s in range(start, stop):
            hi, lo = split(m32[s].T)
            m2[s, :size, :] = hi
            m2[s, size:, :] = lo

    def share(buf, send, recv, o, h):
        return pltpu.make_async_remote_copy(
            src_ref=buf.at[h, me],
            dst_ref=buf.at[h, me],
            send_sem=send.at[o, h],
            recv_sem=recv.at[o, h],
            device_id={"head": lax.rem(me + o, n)},
            device_id_type=MESH,
        )

    rcopy = functools.partial(share, rbuf, rs, rr)
    qcopy = functools.partial(share, sqbuf, qs, qr)

    def w2copy(o, i):
        source = lax.rem(me + n - o, n)
        part = wout.at[source, pl.ds(pl.multiple_of(mine * slab, slab), slab)]
        return pltpu.make_async_remote_copy(
            src_ref=part,
            dst_ref=part,
            send_sem=w2s.at[o, i],
            recv_sem=w2r.at[o, i],
            device_id={"batch": base + lax.rem(mine + i, group)},
            device_id_type=MESH,
        )

    def pair(hi, lo):
        hi, lo = hi.astype(F32), lo.astype(F32)
        top = jnp.concatenate([hi, hi], axis=1)
        low = jnp.concatenate([lo, lo], axis=1)
        return jnp.concatenate([top, low], axis=0).astype(BF16)

    def piece(x, t):
        return x[t * seqs : (t + 1) * seqs]

    ks, vs, fs, us, rds, rfs = [], [], [], [], [], []
    decay = []
    whole = None
    for h in range(HALVES):
        for at, o in enumerate(order):
            xcopy(o, h).wait_recv()
            project(lax.rem(me + n - o, n), h, False)
            if h == 0:
                prepare(seqs * at // (n - 1), seqs * (at + 1) // (n - 1))

        own = slice(h * band, (h + 1) * band)
        p = pacc[own, :]
        f = 0.8 + 0.2 * jax.nn.sigmoid(gacc[own, :] + bias_ref[...])
        q = p[:, :size]
        k = p[:, size : 2 * size]
        v = p[:, 2 * size :]
        k = k * lax.rsqrt(rowsum(k * k) + 1e-06)
        q = q * lax.rsqrt(rowsum(q * q) + 1e-06)
        kbuf[own, :] = k
        qbuf[own, :] = q
        for s in range(seqs):
            at = pl.ds(h * band + s, part, stride=seqs)
            left = pair(*split(jnp.concatenate([kbuf[at, :], qbuf[at, :]], axis=0)))
            r = jnp.dot(left, a2[s], preferred_element_type=F32)
            r = r[: 2 * part] + r[2 * part :]
            akbuf[at, :] = r[:part]
            aqbuf[at, :] = r[part:]

        now = range(h * part, (h + 1) * part)
        ks += [piece(k, t) for t in range(part)]
        vs += [piece(v, t) for t in range(part)]
        fs += [piece(f, t) for t in range(part)]
        qn = {t: piece(q, t - now[0]) for t in now}
        ak = {t: akbuf[t * seqs : (t + 1) * seqs, :] for t in now}
        aq = {t: aqbuf[t * seqs : (t + 1) * seqs, :] for t in now}
        ws = {}
        for t in range(now[-1] + 1):
            if t in now:
                us.append(ak[t])
                rds.append(1.0 / (fs[t] + rowsum(ks[t] * ak[t])))
                rfs.append(1.0 / fs[t])
            u, rd, rf = us[t], rds[t], rfs[t]
            for i in now:
                if i > t:
                    ak[i] = (ak[i] - u * (rowsum(u * ks[i]) * rd)) * rf
                if i >= t:
                    aq[i] = (aq[i] - u * (rowsum(u * qn[i]) * rd)) * rf
            if t in now:
                ws[t] = aq[t]
                wbuf[t * seqs : (t + 1) * seqs, :] = aq[t]

        if h == HALVES - 1:
            for o in range(1, n):
                w1copy(o).wait_recv()
                for i in range(1, group):
                    w2copy(o, i).start()

        for s in range(seqs):
            at = pl.ds(h * band + s, part, stride=seqs)
            r = jnp.dot(pair(*split(wbuf[at, :])), m2[s], preferred_element_type=F32)
            robuf[at, :] = r[:part] + r[part:]

        pieces = []
        for t in now:
            decay = [fs[t] if x is None else x * fs[t] for x in decay] + [None]
            whole = fs[t] if whole is None else whole * fs[t]
            total = whole * robuf[t * seqs : (t + 1) * seqs, :]
            for i in range(t + 1):
                e = rowsum(ks[i] * ws[t])
                total = total + (e * vs[i] if decay[i] is None else (e * decay[i]) * vs[i])
            pieces.append(total)
        ro = jnp.concatenate(pieces, axis=0)
        hi, lo = split(ro * ro)
        squares = jnp.concatenate([hi, lo], axis=1)
        sqbuf[h, me] = lax.dot_general(
            jnp.ones((8, 2 * size), BF16),
            jnp.concatenate([squares] * HALVES, axis=0),
            NT,
            preferred_element_type=F32,
        )
        rbuf[h, me] = (gain_ref[...] * ro).astype(BF16)
        for o in range(1, n):
            rcopy(o, h).start()
            qcopy(o, h).start()

    loads[5].wait()
    for h in range(HALVES):
        acc = jnp.dot(rbuf[h, me], wout[me], preferred_element_type=F32)
        squares = sqbuf[h, me]
        for o in range(1, n):
            source = lax.rem(me + n - o, n)
            rcopy(o, h).wait_recv()
            qcopy(o, h).wait_recv()
            if h == 0:
                for i in range(1, group):
                    w2copy(o, i).wait_recv()
            acc = acc + jnp.dot(rbuf[h, source], wout[source], preferred_element_type=F32)
            squares = squares + sqbuf[h, source]
        scale = lax.rsqrt(squares[:1] / (n * size) + 1e-06)
        scale = jnp.broadcast_to(scale, (size, rows)).T[:band]
        for at in range(0, cols, size):
            out_ref[h * band : (h + 1) * band, at : at + size] = acc[:, at : at + size] * scale

    for o in range(1, n):
        w1copy(o).wait_send()
        for h in range(HALVES):
            xcopy(o, h).wait_send()
            rcopy(o, h).wait_send()
            qcopy(o, h).wait_send()
        for i in range(1, group):
            w2copy(o, i).wait_send()


def local(n, batch, inputs, in_weight, gate_weight, gate_bias, norm_gain, out_weight, inv_gram, value_key):
    steps, seqs, feats = inputs.shape
    d_model, heads, width = in_weight.shape
    size = width // 3
    rows = steps * seqs
    cols = out_weight.shape[1] // n
    assert heads == 1
    group = math.gcd(math.gcd(batch, 8), out_weight.shape[0] // 16)
    anywhere = pl.BlockSpec(memory_space=pl.ANY)
    vmem = pl.BlockSpec(memory_space=pltpu.VMEM)
    dma = pltpu.SemaphoreType.DMA
    out = pl.pallas_call(
        functools.partial(kernel, n, group),
        out_shape=jax.ShapeDtypeStruct((rows, cols), F32),
        in_specs=[
            anywhere,
            anywhere,
            anywhere,
            vmem,
            vmem,
            anywhere,
            anywhere,
            anywhere,
        ],
        out_specs=vmem,
        scratch_shapes=[
            pltpu.VMEM((n, steps, seqs, feats), BF16),
            pltpu.VMEM((d_model, width), BF16),
            pltpu.VMEM((1, d_model), BF16),
            pltpu.VMEM((seqs, size, size), F32),
            pltpu.VMEM((seqs, size, size), F32),
            pltpu.VMEM((seqs, 2 * size, size), BF16),
            pltpu.VMEM((seqs, 2 * size, size), BF16),
            pltpu.VMEM((n, out_weight.shape[0], cols), BF16),
            pltpu.VMEM((rows, width), F32),
            pltpu.VMEM((rows, size), F32),
            pltpu.VMEM((rows, size), F32),
            pltpu.VMEM((rows, size), F32),
            pltpu.VMEM((rows, size), F32),
            pltpu.VMEM((rows, size), F32),
            pltpu.VMEM((rows, size), F32),
            pltpu.VMEM((rows, size), F32),
            pltpu.VMEM((HALVES, n, rows // HALVES, size), BF16),
            pltpu.VMEM((HALVES, n, 8, rows), F32),
            dma((6,)),
            dma((n, HALVES)),
            dma((n, HALVES)),
            dma((n,)),
            dma((n,)),
            dma((n, group)),
            dma((n, group)),
            dma((n, HALVES)),
            dma((n, HALVES)),
            dma((n, HALVES)),
            dma((n, HALVES)),
        ],
        compiler_params=pltpu.CompilerParams(collective_id=0, has_side_effects=True),
    )(
        inputs,
        in_weight.reshape(d_model, width),
        gate_weight.reshape(1, d_model),
        gate_bias.reshape(1, 1),
        norm_gain.reshape(1, size),
        out_weight,
        inv_gram.reshape(seqs, size, size),
        value_key.reshape(seqs, size, size),
    )
    return out.reshape(steps, seqs, cols)


def solution(mesh):
    in_specs = (
        P(None, "batch", "head"),
        P(None, "head", None),
        P(None, "head"),
        P("head"),
        P("head"),
        P("head", None),
        P("batch", "head", None, None),
        P("batch", "head", None, None),
    )
    out_specs = P(None, "batch", "head")
    return jax.shard_map(
        functools.partial(local, mesh.shape["head"], mesh.shape["batch"]),
        mesh=mesh,
        in_specs=in_specs,
        out_specs=out_specs,
        check_vma=False,
    )
```

time: 29.9 us -> 30.7 us (1.027)
  Pallas kernels: 27.4 us -> 28.2 us
    pallas_call x1, Pallas kernels: 27.4 us -> 28.2 us  [local(): pl.pallas_call(functools.partial(kernel, n, group), out_shape=jax.ShapeDt...]
where the time goes in v3:
time: 30.7 us; the launch traced here: 30.5 us
  Pallas kernels  28.2 us (92%)
  local copies, waits for them, and re-layouts  1.67 us (5%)
  between operations  0.66 us (2%)
    pallas_call x1, Pallas kernels, local(): pl.pallas_call(functools.partial(kernel, n, group), out_shape=jax.ShapeDt...  28.2 us
    unnamed x1, local copies, waits for them, and re-layouts  1.67 us

profile of v3, /device:TPU:0, one launch (start us, length us, event | category | flops | bytes accessed | tf_op | source)
XLA Modules:
  0.0 30.5 jit_solution(6698650534612918587)
XLA Ops:
  0.7 28.2 %shard_map.82 = f32[128,512]{1,0:T(8,128)} custom-call(bf16[8,16,512]{2,1,0:T(8,128)(2,1)} %x_hbm.1, bf16[2048,384]{1,0:T(8,128)(2,1)} %bitcast.8, bf16[1,2048]{1,0:T(2,128)(2,1)} %bitcast.12, f32[1,1]{1,0:T(1,128)} %bitcast.7.bias_ref, f32[1,128]{1,0:T(1,128)} %bitcast.13, bf16[128,2048]{1,0:T(8,128)(2,1)} %ow_hbm.1, f32[16,128,128]{2,1,0:T(8,128)} %bitcast.9, ...), custom_call_target="tpu_custom_call" | custom-call | tf_op jit(solution)/shard_map/pallas_call | solution.py:332
  28.8 1.7 %copy.11 = f32[8,16,512]{2,1,0:T(8,128)} copy(f32[8,16,512]{2,1,0:T(8,128)} %bitcast.11) | data formatting | bytes 524288

commit v4 on v2

--- a/solution.py
+++ b/solution.py
@@ -209,23 +209,6 @@
         ws.append(aq[t])
         wbuf[t * seqs : (t + 1) * seqs, :] = aq[t]
 
-    def w2copy(o, i):
-        source = lax.rem(me + n - o, n)
-        part = wout.at[source, pl.ds(pl.multiple_of(mine * slab, slab), slab)]
-        return pltpu.make_async_remote_copy(
-            src_ref=part,
-            dst_ref=part,
-            send_sem=w2s.at[o, i],
-            recv_sem=w2r.at[o, i],
-            device_id={"batch": base + lax.rem(mine + i, group)},
-            device_id_type=MESH,
-        )
-
-    for o in range(1, n):
-        w1copy(o).wait_recv()
-        for i in range(1, group):
-            w2copy(o, i).start()
-
     for s in range(seqs):
         at = pl.ds(s, steps, stride=seqs)
         hi, lo = split(wbuf[at, :])
@@ -274,6 +257,23 @@
         rcopy(o).start()
         qcopy(o).start()
 
+    def w2copy(o, i):
+        source = lax.rem(me + n - o, n)
+        part = wout.at[source, pl.ds(pl.multiple_of(mine * slab, slab), slab)]
+        return pltpu.make_async_remote_copy(
+            src_ref=part,
+            dst_ref=part,
+            send_sem=w2s.at[o, i],
+            recv_sem=w2r.at[o, i],
+            device_id={"batch": base + lax.rem(mine + i, group)},
+            device_id_type=MESH,
+        )
+
+    for o in range(1, n):
+        w1copy(o).wait_recv()
+        for i in range(1, group):
+            w2copy(o, i).start()
+
     loads[5].wait()
     acc = jnp.dot(rbuf[me], wout[me], preferred_element_type=F32)
     squares = sqbuf[me]

time: 29.9 us -> 29.9 us (level)
  no operation moved by 1% of the time
where the time goes in v4:
time: 29.9 us; the launch traced here: 29.7 us
  Pallas kernels  27.4 us (92%)
  local copies, waits for them, and re-layouts  1.67 us (6%)
  between operations  0.66 us (2%)
    pallas_call x1, Pallas kernels, local(): pl.pallas_call(functools.partial(kernel, n, group), out_shape=jax.ShapeDt...  27.4 us
    unnamed x1, local copies, waits for them, and re-layouts  1.67 us

profile of v4, /device:TPU:0, one launch (start us, length us, event | category | flops | bytes accessed | tf_op | source)
XLA Modules:
  0.0 29.7 jit_solution(8241341821692485220)
XLA Ops:
  0.7 27.4 %shard_map.82 = f32[128,512]{1,0:T(8,128)} custom-call(bf16[8,16,512]{2,1,0:T(8,128)(2,1)} %x_hbm.1, bf16[2048,384]{1,0:T(8,128)(2,1)} %bitcast.8, bf16[1,2048]{1,0:T(2,128)(2,1)} %bitcast.12, f32[1,1]{1,0:T(1,128)} %bitcast.7.bias_ref, f32[1,128]{1,0:T(1,128)} %bitcast.13, bf16[128,2048]{1,0:T(8,128)(2,1)} %ow_hbm.1, f32[16,128,128]{2,1,0:T(8,128)} %bitcast.9, ...), custom_call_target="tpu_custom_call" | custom-call | tf_op jit(solution)/shard_map/pallas_call | solution.py:313
  28.0 1.7 %copy.11 = f32[8,16,512]{2,1,0:T(8,128)} copy(f32[8,16,512]{2,1,0:T(8,128)} %bitcast.11) | data formatting | bytes 524288
